TPU v7x, 512 devices: a whole 4x8x8 slice. The times are simulated.
512 devices in a mesh: dp: 64 (over z, y_lo, core), tensor: 8 (over x, y_hi).
Axes of the slice: x: 4, y: 8 (y_hi: 2, y_lo: 4; y = y_hi * 4 + y_lo), z: 8, core: 2. Of those that a mesh axis runs over, the one named last changes fastest.
Arguments:
- attn_out: bfloat16 [49152, 2048], P('dp', 'tensor'), may hold values from -6 to 6
- out_proj_t: bfloat16 [4096, 2048], P(None, 'tensor'), may hold values from -0.09375 to 0.09375
- grad_out: bfloat16 [49152, 4096], P('dp', 'tensor'), may hold values from -16 to 16
- read_weights: float32 [49152, 16], P('dp'), may hold values from 0 to 0.0026041667
- memory_gate: float32 [1024, 16], P('dp'), may hold values from -0.2 to 1
- write_pos: int32 [64, 16], P('dp'), may hold values from 0 to 767, as said below
Outputs:
- grad_attn_out: bfloat16 [49152, 2048], P('dp', 'tensor')
- grad_out_proj_t: float32 [4096, 2048], P('dp', 'tensor')
- grad_memory: float32 [1024, 4096], P('dp', 'tensor')
Inputs may be any that keep to these rules, and one draw needn't show every extreme that they name: `write_pos`: the 16 positions of one segment are distinct.
All inputs are finite; a program needn't handle non-finite values.
Results may differ from a plain program's by a relative error of at most 0.0034.
Values may be sent and summed in bfloat16 or wider, within the bound.
A program may use at most 64 MiB of HBM per device.

v0:
```python
import jax
import jax.numpy as jnp
from jax import lax
from jax.sharding import Mesh
from jax.sharding import PartitionSpec as P

DP = ("dp_0", "dp_1", "dp_2")


def nothing_yet(value, identity):
    return jax.tree.map(
        lambda part, zero: jnp.zeros_like(part) + jnp.asarray(zero, part.dtype), value, identity
    )


def gathered_once(value, axis):
    leaves = jax.tree.leaves(value)
    sequence = sorted(range(len(leaves)), key=lambda k: -leaves[k].size)
    width = (1, *leaves[sequence[0]].shape)[-1]
    lines = [
        jnp.pad(leaves[k].reshape(-1), (0, -leaves[k].size % width)).reshape(-1, width)
        for k in sequence
    ]
    both, at, found = (lax.all_gather(jnp.concatenate(lines), axis), 0, {})
    for k, line in zip(sequence, lines):
        slab = both[:, at : at + len(line)].reshape(len(both), -1)
        found[k] = slab[:, : leaves[k].size].reshape(-1, *leaves[k].shape)
        at += len(line)
    numbers = iter(range(len(leaves)))
    return jax.tree.map(lambda _: found[next(numbers)], value)


def entering(value, axes, combine, identity):
    before = start = nothing_yet(value, identity)
    subtotal = value
    for axis in reversed(axes):
        count, position = (lax.axis_size(axis), lax.axis_index(axis))
        pieces = gathered_once(subtotal, axis)
        inside, subtotal = (start, start)
        for k in reversed(range(count)):
            passed = k > position
            subtotal = combine(subtotal, jax.tree.map(lambda part: part[k], pieces))
            inside = jax.tree.map(lambda new, old: jnp.where(passed, new, old), subtotal, inside)
        before = combine(inside, before)
    return before


def cut_along(value, dim, count):
    before, after = (value.shape[:dim], value.shape[dim + 1 :])
    return jnp.moveaxis(value.reshape(*before, count, -1, *after), dim, 0)


def scatter_pairs(value, chips, core, dim):
    sizes = (lax.axis_size(chips), lax.axis_size(core))
    parts = cut_along(value, dim, sizes[0] * sizes[1])
    inside = parts.shape[1:]
    parts = parts.reshape(*sizes, *inside).swapaxes(0, 1).reshape(-1, *inside)
    parts = lax.psum_scatter(parts, core, scatter_dimension=0, tiled=True)
    return lax.psum_scatter(parts, chips, scatter_dimension=0, tiled=True)[0]


def compose(earlier, later):
    high = lax.Precision.HIGHEST
    gate_early, term_early = earlier
    trailing_gate, term_late = later
    gate = jnp.dot(trailing_gate, gate_early, precision=high, preferred_element_type=jnp.float32)
    term = (
        jnp.dot(trailing_gate, term_early, precision=high, preferred_element_type=jnp.float32)
        + term_late
    )
    return (gate, term)


def body(attn_out, out_proj_t, grad_out, read_weights, memory_gate, write_pos):
    high = lax.Precision.HIGHEST
    seg_len = attn_out.shape[0]
    slots = write_pos.shape[1]
    gate_at_step = memory_gate.T
    dy_cols = grad_out.astype(jnp.float32)
    local = jnp.dot(read_weights.T, dy_cols, precision=high, preferred_element_type=jnp.float32)
    identity = (jnp.eye(slots, dtype=jnp.float32), jnp.zeros_like(local))
    composed = entering((gate_at_step, local), DP, compose, identity)
    after = composed[1]
    grad_memory = (
        jnp.dot(gate_at_step, after, precision=high, preferred_element_type=jnp.float32) + local
    )
    places = jnp.arange(seg_len, dtype=jnp.int32)
    onehot = (places[:, None] == write_pos[0][None, :]).astype(jnp.float32)
    written = jnp.dot(onehot, after, precision=high, preferred_element_type=jnp.float32)
    grad_z = (dy_cols + written).astype(jnp.bfloat16)
    full_z = lax.all_gather(grad_z, "tensor", axis=1, tiled=True)
    grad_attn = jnp.dot(full_z, out_proj_t, preferred_element_type=jnp.float32).astype(jnp.bfloat16)
    term = lax.dot_general(
        full_z, attn_out, (((0,), (0,)), ((), ())), preferred_element_type=jnp.float32
    )
    grad_weight = scatter_pairs(term, ("dp_0", "dp_1"), "dp_2", 0)
    return (grad_attn, grad_weight, grad_memory)


def solution(mesh):
    finer = Mesh(
        mesh.devices.reshape(8, 4, 2, mesh.shape["tensor"]), ("dp_0", "dp_1", "dp_2", "tensor")
    )
    placed = (
        P(DP, "tensor"),
        P(None, "tensor"),
        P(DP, "tensor"),
        P(DP, None),
        P(DP, None),
        P(DP, None),
    )
    return jax.shard_map(
        body,
        mesh=finer,
        in_specs=placed,
        out_specs=(P(DP, "tensor"), P(DP, "tensor"), P(DP, "tensor")),
        check_vma=False,
    )
```

profile of v0, /device:TPU:2, one launch (start us, length us, event | category | flops | bytes accessed | tf_op | source)
XLA Modules:
  0.0 418.0 jit_solution(931132758873933448)
XLA Ops:
  7.2 0.0 copy-start
  7.2 0.0 copy-start.1
  7.2 0.0 copy-start.3
  7.2 0.0 all-gather.8.cloned.1.call-start
  7.3 0.9 copy.12
  8.2 0.1 reshape.73
  8.3 1.6 fusion.43
  9.9 1.9 all-gather.3
  11.8 0.1 squeeze.88
  11.9 0.1 fusion.31
  12.0 0.1 convolution_add_fusion.14
  12.1 0.1 squeeze.87
  12.2 0.1 fusion.44
  12.4 0.1 reshape.76
  12.5 0.2 convolution_add_fusion.13
  12.6 13.9 %all-gather.4 = f32[4,17,512]{2,1,0:T(8,128)S(1)} all-gather(f32[1,17,512]{2,1,0:T(8,128)S(1)} %maximum_bitcast_fusion.1), channel_id=3, replica_groups=mesh['dp_0'=8,'dp_1'=4,'dp_2'=2,'tensor'=8] {'dp_1'}, dimensions={0}, use_global_device_ids=true | all-gather | bytes 174080 | tf_op jit(solution)/shard_map/all_gather | solution.py:24
  26.6 0.1 squeeze.94
  26.7 0.1 fusion.30
  26.8 0.1 convolution_add_fusion.12
  26.9 0.1 squeeze.93
  27.0 0.1 squeeze.92
  27.1 0.1 squeeze.91
  27.2 0.1 fusion.45
  27.3 0.1 fusion.46
  27.4 0.1 fusion.47
  27.6 0.1 reshape.79
  27.7 0.2 convolution_add_fusion.11
  27.9 0.2 convolution_add_fusion.10
  28.0 0.2 convolution_add_fusion.9
  28.2 0.1 fusion.23
  28.3 0.1 fusion.28
  28.5 0.2 fusion.6
  28.7 31.5 %all-gather.5 = f32[8,17,512]{2,1,0:T(8,128)S(1)} all-gather(f32[1,17,512]{2,1,0:T(8,128)S(1)} %maximum_bitcast_fusion.2), channel_id=4, replica_groups=mesh['dp_0'=8,'dp_1'=4,'dp_2'=2,'tensor'=8] {'dp_0'}, dimensions={0}, use_global_device_ids=true | all-gather | bytes 313344 | tf_op jit(solution)/shard_map/all_gather | solution.py:24
  60.2 0.1 squeeze.106
  60.3 0.1 squeeze.105
  60.4 0.1 squeeze.104
  60.4 0.1 squeeze.103
  60.5 0.1 squeeze.102
  60.6 0.1 squeeze.101
  60.7 0.1 squeeze.100
  60.7 0.1 squeeze.99
  60.8 0.2 convolution_add_fusion.8
  61.0 0.2 convolution_add_fusion.7
  61.2 0.2 convolution_add_fusion.6
  61.4 0.2 convolution_add_fusion.5
  61.5 0.2 convolution_add_fusion.4
  61.7 0.2 convolution_add_fusion.3
  61.9 0.2 convolution_add_fusion.2
  62.0 0.2 fusion.2
  62.2 0.1 fusion.48
  62.4 0.2 fusion.1
  62.5 1.7 add_convert_fusion
  64.2 0.0 all-gather.8.cloned.1.call-update
  64.2 0.0 reduce-scatter.3.cloned.1.call-start
  64.3 146.9 %all-gather.8.cloned.1.call-done = bf16[768,4096]{1,0:T(8,128)(2,1)} async-done(((bf16[768,512]{1,0:T(8,128)(2,1)}), bf16[768,4096]{1,0:T(8,128)(2,1)}) %all-gather.8.cloned.1.call-update) | async-done | bytes 6291472 | tf_op jit(solution)/shard_map/all_gather | solution.py:91
  211.2 4.7 %fusion.49 = f32[4096,256]{1,0:T(8,128)S(1)} fusion(bf16[768,4096]{1,0:T(8,128)(2,1)} %all-gather.8.cloned.1.call-done, bf16[768,256]{1,0:T(8,128)(2,1)} %param.6), kind=kOutput, calls=%fused_computation.103 | convolution fusion | flops 1610612736 | bytes 10878976 | tf_op jit(solution)/shard_map/dot_general | solution.py:93
  216.0 2.3 copy.13
  218.3 0.0 reduce-scatter.3.cloned.1.call-update
  218.4 0.0 reduce-scatter.5.cloned.1.call-start
  218.4 19.7 %reduce-scatter.3.cloned.1.call-done = f32[32,64,256]{2,1,0:T(8,128)} async-done(((f32[64,64,256]{2,1,0:T(8,128)}), f32[32,64,256]{2,1,0:T(8,128)}) %reduce-scatter.3.cloned.1.call-update) | async-done | bytes 2097168 | tf_op jit(solution)/shard_map/reduce_scatter | solution.py:58
  238.1 0.0 reduce-scatter.5.cloned.1.call-update
  238.1 0.8 fusion
  239.0 5.3 %convolution_convert_fusion = bf16[768,256]{1,0:T(8,128)(2,1)} fusion(bf16[768,4096]{1,0:T(8,128)(2,1)} %all-gather.8.cloned.1.call-done, bf16[4096,256]{1,0:T(8,128)(2,1)S(1)} %copy-done), kind=kOutput, calls=%fused_computation.1 | convolution fusion | flops 1610809344 | bytes 8781824 | tf_op jit(solution)/shard_map/dot_general | solution.py:92
  244.3 167.2 %reduce-scatter.5.cloned.1.call-done = f32[1,64,256]{2,1,0:T(8,128)} async-done(((f32[32,64,256]{2,1,0:T(8,128)}), f32[1,64,256]{2,1,0:T(8,128)}) %reduce-scatter.5.cloned.1.call-update) | async-done | bytes 65552 | tf_op jit(solution)/shard_map/reduce_scatter | solution.py:59
  (20 shorter events, 0.2 us)
Async XLA Ops:
  7.2 231.8 %copy-start = (bf16[4096,256]{1,0:T(8,128)(2,1)S(1)}, bf16[4096,256]{1,0:T(8,128)(2,1)}, u32[]{:S(2)}) copy-start(bf16[4096,256]{1,0:T(8,128)(2,1)} %param.7) | copy-start | bytes 6291460
  7.2 55.3 %copy-start.1 = (bf16[768,512]{1,0:T(8,128)(2,1)S(1)}, bf16[768,512]{1,0:T(8,128)(2,1)}, u32[]{:S(2)}) copy-start(bf16[768,512]{1,0:T(8,128)(2,1)} %param.8) | copy-start | bytes 2359300
  7.2 55.3 %copy-start.3 = (s32[1,16]{1,0:T(1,128)S(1)}, s32[1,16]{1,0:T(1,128)}, u32[]{:S(2)}) copy-start(s32[1,16]{1,0:T(1,128)} %param.11) | copy-start | bytes 196
  7.2 204.0 %all-gather.8.cloned.1.call-start = ((), (), s32[]{:S(2)}) async-start(), calls=%async_computation.2 | async-start | bytes 7077888 | tf_op jit(solution)/shard_map/all_gather | solution.py:91
  64.2 173.8 %reduce-scatter.3.cloned.1.call-start = ((), (), s32[]{:S(2)}) async-start(), calls=%async_computation.3 | async-start | bytes 6291456 | tf_op jit(solution)/shard_map/reduce_scatter | solution.py:58
  218.3 19.8 %copy-start.2 = (f32[16,16]{1,0:T(8,128)S(1)}, f32[16,16]{1,0:T(8,128)}, u32[]{:S(2)}) copy-start(f32[16,16]{1,0:T(8,128)} %param.10) | copy-start | bytes 3076
  218.4 193.1 %reduce-scatter.5.cloned.1.call-start = ((), (), s32[]{:S(2)}) async-start(), calls=%async_computation.4 | async-start | bytes 2162688 | tf_op jit(solution)/shard_map/reduce_scatter | solution.py:59
Sparse Core Ops, SparseCore 0:
  64.4 146.8 all-gather.7
  218.5 19.5 reduce-scatter.2
  241.5 169.9 reduce-scatter.4
where the time goes:
time: 418 us
  waiting for transfers between devices  334 us (80%)
  blocking collectives  47.3 us (11%)
  matrix products  18 us (4%)
  between operations  14 us (3%)
  local copies, waits for them, and re-layouts  4.76 us (1%)
    reduce_scatter x1, waiting for transfers between devices, scatter_pairs(): return lax.psum_scatter(parts, chips, scatter_dimension=0, tiled=True)[0]  167 us
    all_gather x1, waiting for transfers between devices, body(): full_z = lax.all_gather(grad_z, 'tensor', axis=1, tiled=True)  147 us
    all_gather x3, blocking collectives, gathered_once(): both, at, found = (lax.all_gather(jnp.concatenate(lines), axis), 0, {})  47.3 us
    reduce_scatter x1, waiting for transfers between devices, scatter_pairs(): parts = lax.psum_scatter(parts, core, scatter_dimension=0, tiled=True)  19.7 us
  transfers between devices with their start and end apart: 3, of which 3 were waited for; matrix products, arithmetic and copies ran while one was open for 1% of the time, Pallas kernels for 0%

commit v1 on v0

v1 whole, which is shorter than its diff:
```python
import functools

import jax
import jax.numpy as jnp
from jax import lax
from jax.experimental import pallas as pl
from jax.experimental.pallas import tpu as pltpu
from jax.sharding import PartitionSpec as P

T, DS, HS, MEM = 768, 512, 256, 16
XCH, XROWS = 3, 256
YCH, YROWS = 4, 192
F32, BF16 = jnp.float32, jnp.bfloat16
HIGH = lax.Precision.HIGHEST
SUM0 = (((0,), (0,)), ((), ()))


def tdot(a, b, precision=None):
    return lax.dot_general(a, b, SUM0, precision=precision, preferred_element_type=F32)


def dot(a, b):
    return jnp.dot(a, b, preferred_element_type=F32)


def parts3(v):
    hi = v.astype(BF16)
    rest = v - hi.astype(F32)
    mid = rest.astype(BF16)
    return hi, mid, (rest - mid.astype(F32)).astype(BF16)


def apply_map(m, v):
    out = m[:, 0:1] * v[0:1, :]
    for k in range(1, MEM):
        out = out + m[:, k : k + 1] * v[k : k + 1, :]
    return out


def kernel(
    g, attn, w, rw, gate, wp, oa, ow, om,
    G, A, ARelay, WP, S1, S2, S3, vr, R, Rows, acc, Ps, PRelay, Pr, Pf, Cs, Cr, Ss, Zr, Ys, Yr, oh,
    xs, xr, fs, fr, as1, ar1, as2, ar2, w1, wzs, wzr, wc, l1, l2s, l2r, l3s, l3r, rs, rr,
    ps1, pr1, ps2, pr2, cs, cr, zs, zr, ys, yr,
):
    dp, tp = lax.axis_index("dp"), lax.axis_index("tensor")
    z, yl, c = lax.div(dp, 8), lax.rem(lax.div(dp, 2), 4), lax.rem(dp, 2)
    x, yh = lax.div(tp, 2), lax.rem(tp, 2)
    y = 4 * yh + yl

    def dev(x_=None, y_=None, z_=None, c_=None):
        x_ = x if x_ is None else x_
        y_ = y if y_ is None else y_
        z_ = z if z_ is None else z_
        c_ = c if c_ is None else c_
        return (8 * z_ + 2 * lax.rem(y_, 4) + c_, 2 * x_ + lax.div(y_, 4))

    def copy(src, dst, send, recv, to):
        return pltpu.make_async_remote_copy(
            src_ref=src, dst_ref=dst, send_sem=send, recv_sem=recv,
            device_id=to, device_id_type=pl.DeviceIdType.MESH,
        )

    xn = [lax.rem(x + k, 4) for k in range(4)]
    right, left, across = dev(x_=xn[1]), dev(x_=xn[3]), dev(x_=xn[2])
    yn = [lax.rem(y + k, 8) for k in range(8)]
    up, down, far = dev(y_=yn[2]), dev(y_=yn[6]), dev(y_=yn[4])
    mate = dev(c_=1 - c)
    lo = [dev(y_=4 * yh + lax.rem(yl + k, 4)) for k in range(4)]
    zn = [lax.rem(z + k, 8) for k in range(8)]
    zdev = [dev(z_=zn[k]) for k in range(8)]
    odd = lax.rem(z, 2)
    zx = z + 1 - 2 * odd
    straight = odd == yh
    cross = [dev(y_=4 * (1 - yh) + lax.rem(yl + k, 4), z_=zx) for k in range(4)]

    barrier = pltpu.get_barrier_semaphore()
    greeted = [right, left, across, up, down, far, mate] + lo[1:] + zdev[1:] + cross
    for peer in greeted:
        pl.semaphore_signal(barrier, inc=1, device_id=peer, device_id_type=pl.DeviceIdType.MESH)
    pl.semaphore_wait(barrier, len(greeted))

    sent = []

    def go(d):
        d.start()
        sent.append(d)

    def own_right(k):
        r = pl.ds(k * XROWS, XROWS)
        return copy(g.at[r], G.at[2, r], xs.at[0, k], xr.at[0, k], right)

    def own_left(k):
        r = pl.ds(k * XROWS, XROWS)
        return copy(g.at[r], G.at[0, r], xs.at[1, k], xr.at[1, k], left)

    half = XROWS // 2

    def on_right(k):
        r = pl.ds(k * XROWS, half)
        return copy(G.at[2, r], G.at[1, r], fs.at[0, k], fr.at[0, k], right)

    def on_left(k):
        r = pl.ds(k * XROWS + half, half)
        return copy(G.at[0, r], G.at[1, r], fs.at[1, k], fr.at[1, k], left)

    def ydir(j):
        return up if j < YCH // 2 else down

    def attn_first(j):
        r = pl.ds(j * YROWS, YROWS)
        return copy(attn.at[r], ARelay.at[j], as1.at[j], ar1.at[j], ydir(j))

    def attn_second(j):
        origin = yn[6] if j < YCH // 2 else yn[2]
        cols = pl.ds(pl.multiple_of(lax.div(origin, 4) * HS, HS), HS)
        r = pl.ds(j * YROWS, YROWS)
        return copy(ARelay.at[j], A.at[r, cols], as2.at[j], ar2.at[j], ydir(j))

    for k in range(XCH):
        go(own_right(k))
        go(own_left(k))
    go(attn_first(0))
    go(attn_first(2))
    wrow = pl.multiple_of((2 * (2 * c + lax.div(z, 4)) + 1 - yh) * DS + lax.rem(z, 4) * 128, 128)
    wpiece = pl.ds(pl.multiple_of(c * 1024 + z * 128, 128), 128)
    wfirst = copy(w.at[pl.ds(wrow, 128)], WP.at[wpiece], w1.at[0], w1.at[1], far)
    go(wfirst)

    picks = lax.broadcasted_iota(jnp.int32, (T, MEM), 0) == wp[...]
    oh[...] = picks.astype(F32).astype(BF16)
    gv = g[...]
    hi, mid, low = parts3(rw[...])
    local = tdot(low, gv) + tdot(mid, gv) + tdot(hi, gv)
    eye = (
        lax.broadcasted_iota(jnp.int32, (MEM, 128), 0)
        == lax.broadcasted_iota(jnp.int32, (MEM, 128), 1)
    ).astype(F32)
    S1[c, :, :DS] = local
    S1[c, :, DS:] = tdot(gate[...], eye, HIGH)
    lcopy = copy(S1.at[c], S1.at[c], l1.at[0], l1.at[1], mate)
    go(lcopy)
    grows = tdot(oh[...], gv)
    own_cols = pl.ds(pl.multiple_of(yh * HS, HS), HS)
    A[:, own_cols] = attn[...]

    def compose(early, late):
        both = apply_map(early[:, DS:], late)
        return both[:, :DS] + early[:, :DS], both[:, DS:]

    lcopy.wait_recv()
    term, mat = compose(S1[0], S1[1])
    S2[yl, :, :DS] = term
    S2[yl, :, DS:] = mat
    for k in range(1, 4):
        go(copy(S2.at[yl], S2.at[yl], l2s.at[k], l2r.at[yl], lo[k]))
    go(attn_first(1))
    go(attn_first(3))
    for k in range(1, 4):
        slot = lax.rem(yl + k, 4)
        copy(S2.at[slot], S2.at[slot], l2s.at[k], l2r.at[slot], lo[k]).wait_recv()
    term, mat = compose(S2[2], S2[3])
    for k in (1, 0):
        term, mat = compose(S2[k], jnp.concatenate([term, mat], axis=1))
    S3[z, :, :DS] = term
    S3[z, :, DS:] = mat
    for zz in range(7):
        @pl.when(zz < z)
        def _():
            copy(S3.at[z], S3.at[z], l3s.at[zz], l3r.at[z], dev(z_=zz)).start()

    for j in (0, 2):
        attn_first(j).wait_recv()
        go(attn_second(j))
    wfirst.wait_recv()

    def wspread(k):
        piece = pl.ds(pl.multiple_of(c * 1024 + zn[k] * 128, 128), 128)
        return copy(WP.at[piece], WP.at[piece], wzs.at[k], wzr.at[zn[k]], zdev[k])

    for k in (1, 7, 2, 6, 3, 5, 4):
        go(copy(WP.at[wpiece], WP.at[wpiece], wzs.at[k], wzr.at[z], zdev[k]))
    for j in (1, 3):
        attn_first(j).wait_recv()
        go(attn_second(j))

    vr[...] = jnp.zeros((MEM, DS), F32)

    def through(s):
        vr[...] = apply_map(s[:, DS:], vr[...]) + s[:, :DS]

    for zz in range(7, 0, -1):
        @pl.when(zz > z)
        def _():
            copy(S3.at[zz], S3.at[zz], l3s.at[0], l3r.at[zz], dev(z_=zz)).wait_recv()
            through(S3[zz])

    for k in range(3, 0, -1):
        @pl.when(k > yl)
        def _():
            through(S2[k])

    @pl.when(c == 0)
    def _():
        through(S1[1])

    after = vr[...]
    mine = S1[c]
    om[...] = apply_map(mine[:, DS:], after) + mine[:, :DS]
    R[0, :MEM] = (grows + after).astype(BF16)
    R[0, MEM:] = (-grows).astype(BF16)

    def rcopy(k):
        return copy(R.at[0], R.at[4 - k], rs.at[k], rr.at[4 - k], (right, across, left)[k - 1])

    for k in (1, 3, 2):
        go(rcopy(k))
    for k in range(XCH):
        own_right(k).wait_recv()
        go(on_right(k))
        own_left(k).wait_recv()
        go(on_left(k))
    for k in range(1, 8):
        wspread(k).wait_recv()
    chalf = pl.ds(pl.multiple_of(c * 1024, 1024), 1024)
    ohalf = pl.ds(pl.multiple_of((1 - c) * 1024, 1024), 1024)
    go(copy(WP.at[chalf], WP.at[chalf], wc.at[0], wc.at[1], mate))

    def rows_of(rel):
        return g if rel == 0 else G.at[rel - 1]

    def forward(rel, which, first):
        src = rows_of(rel)
        if which == 0:
            weight = w[pl.ds(pl.multiple_of((2 * xn[rel] + yh) * DS, DS), DS), :]
        else:
            weight = WP[pl.ds(pl.multiple_of(xn[rel] * DS, DS), DS), :]
        for b in range(3):
            r = pl.ds(b * 256, 256)
            part = dot(src[r, :], weight)
            acc[which, r, :] = part if first else acc[which, r, :] + part

    def gradient(rel):
        src = rows_of(rel)
        for b in range(2):
            cols = pl.ds(b * 256, 256)
            Pf[rel, cols, :] = tdot(src[:, cols], A[...]) + tdot(R[rel, :, cols], Rows[...])
        for k in range(4):
            theirs = pl.ds(pl.multiple_of((2 * k + 1 - c) * 64, 64), 64)
            Cs[rel, k * 64 : k * 64 + 64, :] = Pf[rel, theirs, :].astype(BF16)
        go(ccopy(rel))

    def ccopy(rel):
        return copy(Cs.at[rel], Cr.at[rel], cs.at[rel], cr.at[rel], mate)

    def zsend(rel, q):
        return copy(
            Ss.at[rel, q], Zr.at[z], zs.at[rel, q], zr.at[z], dev(z_=2 * xn[rel] + q)
        )

    def scatter(rel):
        ccopy(rel).wait_recv()
        for k in range(4):
            ours = pl.ds(pl.multiple_of((2 * k + c) * 64, 64), 64)
            part = slice(k * 64, k * 64 + 64)
            total = (Pf[rel, ours, :] + Cr[rel, part, :].astype(F32)).astype(BF16)
            Ss[rel, 0, part, :] = total[:, :HS]
            Ss[rel, 1, part, :] = total[:, HS:]
        for q in range(2):
            @pl.when(2 * xn[rel] + q != z)
            def _():
                zsend(rel, q).start()

            @pl.when(2 * xn[rel] + q == z)
            def _():
                Zr[z] = Ss[rel, q]

    forward(0, 0, True)
    for j in range(YCH):
        attn_second(j).wait_recv()
    arows = tdot(oh[...], A[...]).astype(BF16)
    Rows[:MEM] = arows
    Rows[MEM:] = arows
    gradient(0)
    copy(WP.at[ohalf], WP.at[ohalf], wc.at[0], wc.at[1], mate).wait_recv()
    forward(0, 1, True)
    scatter(0)
    for k in (3, 1):
        rcopy(k).wait_recv()
        gradient(4 - k)
        forward(4 - k, 0, False)
        forward(4 - k, 1, False)
        scatter(4 - k)
    rcopy(2).wait_recv()
    for k in range(XCH):
        on_right(k).wait_recv()
        on_left(k).wait_recv()
    forward(2, 1, False)

    def change(which):
        total = None
        for rel in range(4):
            if which == 0:
                weight = w[pl.ds(pl.multiple_of((2 * xn[rel] + yh) * DS, DS), DS), :]
            else:
                weight = WP[pl.ds(pl.multiple_of(xn[rel] * DS, DS), DS), :]
            part = dot(R[rel], weight)
            total = part if total is None else total + part
        hi, mid, low = parts3(total[:MEM] + total[MEM:])
        o = oh[...]
        return dot(o, hi) + dot(o, mid) + dot(o, low)

    Ps[...] = (acc[1] + change(1)).astype(BF16)

    def part_first(j):
        r = pl.ds(j * YROWS, YROWS)
        return copy(Ps.at[r], PRelay.at[j], ps1.at[j], pr1.at[j], ydir(j))

    def part_second(j):
        r = pl.ds(j * YROWS, YROWS)
        return copy(PRelay.at[j], Pr.at[r], ps2.at[j], pr2.at[j], ydir(j))

    gradient(2)
    for j in (0, 2, 1, 3):
        go(part_first(j))
    scatter(2)
    forward(2, 0, False)
    acc[0] = acc[0] + change(0)
    for j in (0, 2, 1, 3):
        part_first(j).wait_recv()
        go(part_second(j))

    for zz in range(8):
        @pl.when(zz != z)
        def _():
            copy(Zr.at[zz], Zr.at[zz], zs.at[0, 0], zr.at[zz], dev(z_=zz)).wait_recv()

    total = Zr[0].astype(F32)
    for zz in range(1, 8):
        total = total + Zr[zz].astype(F32)
    for k in range(4):
        Ys[k] = total[k * 64 : k * 64 + 64].astype(BF16)

    zf = jnp.where(straight, z, zx)
    yhf = jnp.where(straight, yh, 1 - yh)

    def ysend(k):
        there = lax.rem(yl + k, 4)
        return copy(Ys.at[there], Yr.at[yl], ys.at[k], yr.at[yl], dev(y_=4 * yhf + there, z_=zf))

    for k in range(1, 4):
        go(ysend(k))

    @pl.when(straight)
    def _():
        Yr[yl] = Ys[yl]

    @pl.when(jnp.logical_not(straight))
    def _():
        ysend(0).start()

    for j in (0, 2, 1, 3):
        part_second(j).wait_recv()
    oa[...] = (acc[0] + Pr[...].astype(F32)).astype(BF16)

    for k in range(1, 4):
        slot = lax.rem(yl + k, 4)
        copy(Ys.at[0], Yr.at[slot], ys.at[k], yr.at[slot], lo[k]).wait_recv()

    @pl.when(jnp.logical_not(straight))
    def _():
        d = ysend(0)
        d.wait_send()
        d.wait_recv()

    ow[...] = (Yr[0].astype(F32) + Yr[1].astype(F32)) + (Yr[2].astype(F32) + Yr[3].astype(F32))

    for d in sent:
        d.wait_send()
    for zz in range(7):
        @pl.when(zz < z)
        def _():
            copy(S3.at[z], S3.at[z], l3s.at[zz], l3r.at[z], dev(z_=zz)).wait_send()
    for rel in range(4):
        for q in range(2):
            @pl.when(2 * xn[rel] + q != z)
            def _():
                zsend(rel, q).wait_send()


def body(attn_out, out_proj_t, grad_out, read_weights, memory_gate, write_pos):
    vm = pl.BlockSpec(memory_space=pltpu.VMEM)
    V, D = pltpu.VMEM, pltpu.SemaphoreType.DMA
    scratch = [
        V((3, T, DS), BF16), V((T, 2 * HS), BF16), V((YCH, YROWS, HS), BF16), V((2048, HS), BF16),
        V((2, MEM, DS + 128), F32), V((4, MEM, DS + 128), F32), V((8, MEM, DS + 128), F32),
        V((MEM, DS), F32), V((4, 2 * MEM, DS), BF16), V((2 * MEM, 2 * HS), BF16),
        V((2, T, HS), F32), V((T, HS), BF16), V((YCH, YROWS, HS), BF16), V((T, HS), BF16),
        V((4, DS, 2 * HS), F32), V((4, 256, 2 * HS), BF16), V((4, 256, 2 * HS), BF16),
        V((4, 2, 256, HS), BF16), V((8, 256, HS), BF16), V((4, 64, HS), BF16), V((4, 64, HS), BF16),
        V((T, MEM), BF16),
        D((2, XCH)), D((2, XCH)), D((2, XCH)), D((2, XCH)),
        D((YCH,)), D((YCH,)), D((YCH,)), D((YCH,)),
        D((2,)), D((8,)), D((8,)), D((2,)), D((2,)), D((4,)), D((4,)), D((8,)), D((8,)),
        D((4,)), D((4,)), D((YCH,)), D((YCH,)), D((YCH,)), D((YCH,)),
        D((4,)), D((4,)), D((4, 2)), D((8,)), D((4,)), D((4,)),
    ]
    return pl.pallas_call(
        kernel,
        out_shape=(
            jax.ShapeDtypeStruct((T, HS), BF16),
            jax.ShapeDtypeStruct((64, HS), F32),
            jax.ShapeDtypeStruct((MEM, DS), F32),
        ),
        in_specs=[vm] * 6,
        out_specs=(vm,) * 3,
        scratch_shapes=scratch,
        compiler_params=pltpu.CompilerParams(
            collective_id=0, has_side_effects=True, vmem_limit_bytes=60 * 1024 * 1024
        ),
    )(grad_out, attn_out, out_proj_t, read_weights, memory_gate, write_pos)


def solution(mesh):
    placed = (
        P("dp", "tensor"), P(None, "tensor"), P("dp", "tensor"),
        P("dp", None), P("dp", None), P("dp", None),
    )
    return jax.shard_map(
        body, mesh=mesh, in_specs=placed,
        out_specs=(P("dp", "tensor"), P("dp", "tensor"), P("dp", "tensor")), check_vma=False,
    )
```

time: 418 us -> 107 us (0.26)
  the two profiles are of different devices: /device:TPU:2 before, /device:TPU:49 now
where the time goes in v1:
time: 107 us
  Pallas kernels  99.8 us (93%)
  local copies, waits for them, and re-layouts  6.33 us (6%)
    pallas_call x1, Pallas kernels, body(): pl.pallas_call(kernel, out_shape=(jax.ShapeDtypeStruct((T, HS), BF16), ja...  99.8 us
    unnamed x4, local copies, waits for them, and re-layouts  6.33 us

profile of v1, /device:TPU:49, one launch (start us, length us, event | category | flops | bytes accessed | tf_op | source)
XLA Modules:
  0.0 106.7 jit_solution(1114975758158429375)
XLA Ops:
  0.6 1.7 %copy.9.rw = f32[768,16]{1,0:T(8,128)} copy(f32[768,16]{0,1:T(8,128)} %param.9) | data formatting | bytes 98304 | tf_op args[3]
  2.3 99.8 %shard_map.85 = (bf16[768,256]{1,0:T(8,128)(2,1)}, f32[64,256]{1,0:T(8,128)}, f32[16,512]{1,0:T(8,128)}) custom-call(bf16[768,512]{1,0:T(8,128)(2,1)} %g.1, bf16[768,256]{1,0:T(8,128)(2,1)} %attn.1, bf16[4096,256]{1,0:T(8,128)(2,1)} %w.1, f32[768,16]{1,0:T(8,128)} %copy.9.rw, f32[16,16]{1,0:T(8,128)} %gate.1, s32[1,16]{1,0:T(1,128)} %wp.1), custom_call_target="tpu_custom_call" | custom-call | tf_op jit(solution)/shard_map/pallas_call | solution.py:408
  102.1 1.8 %copy.13 = bf16[768,256]{1,0:T(8,128)(2,1)} copy(bf16[768,256]{1,0:T(8,128)(2,1)} %get-tuple-element.6) | data formatting | bytes 786432
  103.9 1.5 %copy.14 = f32[64,256]{1,0:T(8,128)} copy(f32[64,256]{1,0:T(8,128)} %get-tuple-element.7) | data formatting | bytes 131072
  105.3 1.4 %copy.15 = f32[16,512]{1,0:T(8,128)} copy(f32[16,512]{1,0:T(8,128)} %get-tuple-element.8) | data formatting | bytes 65536

commit v2 on v1

v2 whole, which is shorter than its diff:
```python
import functools

import jax
import jax.numpy as jnp
from jax import lax
from jax.experimental import pallas as pl
from jax.experimental.pallas import tpu as pltpu
from jax.sharding import PartitionSpec as P

T, DS, HS, MEM = 768, 512, 256, 16
XCH, XROWS = 3, 256
YCH, YROWS = 3, 256
F32, BF16 = jnp.float32, jnp.bfloat16
HIGH = lax.Precision.HIGHEST
SUM0 = (((0,), (0,)), ((), ()))


def tdot(a, b, precision=None):
    return lax.dot_general(a, b, SUM0, precision=precision, preferred_element_type=F32)


def dot(a, b):
    return jnp.dot(a, b, preferred_element_type=F32)


def parts3(v):
    hi = v.astype(BF16)
    rest = v - hi.astype(F32)
    mid = rest.astype(BF16)
    return hi, mid, (rest - mid.astype(F32)).astype(BF16)


def apply_map(m, v):
    out = m[:, 0:1] * v[0:1, :]
    for k in range(1, MEM):
        out = out + m[:, k : k + 1] * v[k : k + 1, :]
    return out


def kernel(
    g_in, attn, w_in, rwt_in, gate_in, wp_in, oa, ow, om,
    g, w, rwt, gate, wp, G, A, WP, S1, S2, S3, vr, R, Rows, acc, Ps, Pr, Pf, Cs, Cr, Ss, Zr, Ys, Yr, oh,
    ins, xs, xr, fs, fr, ats, atr, w1, wzs, wzr, wc, l1, l2s, l2r, l3s, l3r, rs, rr,
    ps, pr, cs, cr, zs, zr, ys, yr,
):
    dp, tp = lax.axis_index("dp"), lax.axis_index("tensor")
    z, yl, c = lax.div(dp, 8), lax.rem(lax.div(dp, 2), 4), lax.rem(dp, 2)
    x, yh = lax.div(tp, 2), lax.rem(tp, 2)
    y = 4 * yh + yl

    def dev(x_=None, y_=None, z_=None, c_=None):
        x_ = x if x_ is None else x_
        y_ = y if y_ is None else y_
        z_ = z if z_ is None else z_
        c_ = c if c_ is None else c_
        return (8 * z_ + 2 * lax.rem(y_, 4) + c_, 2 * x_ + lax.div(y_, 4))

    def copy(src, dst, send, recv, to):
        return pltpu.make_async_remote_copy(
            src_ref=src, dst_ref=dst, send_sem=send, recv_sem=recv,
            device_id=to, device_id_type=pl.DeviceIdType.MESH,
        )

    xn = [lax.rem(x + k, 4) for k in range(4)]
    right, left, across = dev(x_=xn[1]), dev(x_=xn[3]), dev(x_=xn[2])
    yn = [lax.rem(y + k, 8) for k in range(8)]
    far = dev(y_=yn[4])
    mate = dev(c_=1 - c)
    lo = [dev(y_=4 * yh + lax.rem(yl + k, 4)) for k in range(4)]
    zn = [lax.rem(z + k, 8) for k in range(8)]
    zdev = [dev(z_=zn[k]) for k in range(8)]
    odd = lax.rem(z, 2)
    zx = z + 1 - 2 * odd
    straight = odd == yh
    cross = [dev(y_=4 * (1 - yh) + lax.rem(yl + k, 4), z_=zx) for k in range(4)]

    barrier = pltpu.get_barrier_semaphore()
    greeted = [right, left, across, far, mate] + lo[1:] + zdev[1:] + cross
    for peer in greeted:
        pl.semaphore_signal(barrier, inc=1, device_id=peer, device_id_type=pl.DeviceIdType.MESH)

    loads = [
        pltpu.make_async_copy(wp_in, wp, ins.at[6]),
        pltpu.make_async_copy(gate_in, gate, ins.at[7]),
        pltpu.make_async_copy(rwt_in, rwt, ins.at[8]),
        pltpu.make_async_copy(g_in, g, ins.at[0]),
        pltpu.make_async_copy(attn, A.at[0], ins.at[1]),
    ]
    for k in range(4):
        block = pl.ds(pl.multiple_of((2 * k + yh) * DS, DS), DS)
        loads.append(pltpu.make_async_copy(w_in.at[block], w.at[pl.ds(k * DS, DS)], ins.at[2 + k]))
    for load in loads:
        load.start()

    loads[0].wait()
    picks = lax.broadcasted_iota(jnp.int32, (T, MEM), 0) == wp[...]
    oh[...] = picks.astype(F32).astype(BF16)
    eye = (
        lax.broadcasted_iota(jnp.int32, (MEM, 128), 0)
        == lax.broadcasted_iota(jnp.int32, (MEM, 128), 1)
    ).astype(F32)
    loads[1].wait()
    S1[c, :, DS:] = tdot(gate[...], eye, HIGH)
    loads[2].wait()
    hi, mid, low = parts3(rwt[...])
    loads[3].wait()
    gv = g[...]
    S1[c, :, :DS] = dot(low, gv) + dot(mid, gv) + dot(hi, gv)
    pl.semaphore_wait(barrier, len(greeted))

    sent = []

    def go(d):
        d.start()
        sent.append(d)

    lcopy = copy(S1.at[c], S1.at[c], l1.at[0], l1.at[1], mate)
    go(lcopy)

    def own_right(k):
        r = pl.ds(k * XROWS, XROWS)
        return copy(g.at[r], G.at[2, r], xs.at[0, k], xr.at[0, k], right)

    def own_left(k):
        r = pl.ds(k * XROWS, XROWS)
        return copy(g.at[r], G.at[0, r], xs.at[1, k], xr.at[1, k], left)

    half = XROWS // 2

    def on_right(k):
        r = pl.ds(k * XROWS, half)
        return copy(G.at[2, r], G.at[1, r], fs.at[0, k], fr.at[0, k], right)

    def on_left(k):
        r = pl.ds(k * XROWS + half, half)
        return copy(G.at[0, r], G.at[1, r], fs.at[1, k], fr.at[1, k], left)

    def attn_far(j):
        r = pl.ds(j * YROWS, YROWS)
        return copy(A.at[0, r], A.at[1, r], ats.at[j], atr.at[j], far)

    for k in range(XCH):
        go(own_right(k))
        go(own_left(k))
    part = lax.rem(z, 4)
    wrow = pl.multiple_of(
        (2 * (2 * c + lax.div(part, 2)) + 1 - yh) * DS + lax.rem(part, 2) * 256, 256
    )

    def wpart(k):
        return pl.ds(pl.multiple_of(c * 1024 + lax.rem(z + k, 4) * 256, 256), 256)

    wfirst = copy(w_in.at[pl.ds(wrow, 256)], WP.at[wpart(0)], w1.at[0], w1.at[1], far)

    def compose(early, late):
        both = apply_map(early[:, DS:], late)
        return both[:, :DS] + early[:, :DS], both[:, DS:]

    lcopy.wait_recv()
    term, mat = compose(S1[0], S1[1])
    S2[yl, :, :DS] = term
    S2[yl, :, DS:] = mat
    for k in range(1, 4):
        go(copy(S2.at[yl], S2.at[yl], l2s.at[k], l2r.at[yl], lo[k]))
    loads[4].wait()
    grows = tdot(oh[...], gv)
    for k in range(1, 4):
        slot = lax.rem(yl + k, 4)
        copy(S2.at[slot], S2.at[slot], l2s.at[k], l2r.at[slot], lo[k]).wait_recv()
    term, mat = compose(S2[2], S2[3])
    for k in (1, 0):
        term, mat = compose(S2[k], jnp.concatenate([term, mat], axis=1))
    S3[z, :, :DS] = term
    S3[z, :, DS:] = mat
    for zz in range(7):
        @pl.when(zz < z)
        def _():
            copy(S3.at[z], S3.at[z], l3s.at[zz], l3r.at[z], dev(z_=zz)).start()

    go(wfirst)
    for j in range(YCH):
        go(attn_far(j))

    vr[...] = jnp.zeros((MEM, DS), F32)

    def through(s):
        vr[...] = apply_map(s[:, DS:], vr[...]) + s[:, :DS]

    for zz in range(7, 0, -1):
        @pl.when(zz > z)
        def _():
            copy(S3.at[zz], S3.at[zz], l3s.at[0], l3r.at[zz], dev(z_=zz)).wait_recv()
            through(S3[zz])

    for k in range(3, 0, -1):
        @pl.when(k > yl)
        def _():
            through(S2[k])

    @pl.when(c == 0)
    def _():
        through(S1[1])

    after = vr[...]
    mine = S1[c]
    om[...] = apply_map(mine[:, DS:], after) + mine[:, :DS]
    R[0, :MEM] = (grows + after).astype(BF16)
    R[0, MEM:] = (-grows).astype(BF16)

    def rcopy(k):
        return copy(R.at[0], R.at[4 - k], rs.at[k], rr.at[4 - k], (right, across, left)[k - 1])

    for k in (1, 3, 2):
        go(rcopy(k))
    def rows_of(rel):
        return g if rel == 0 else G.at[rel - 1]

    def forward(rel, which, first):
        src = rows_of(rel)
        if which == 0:
            weight = w[pl.ds(pl.multiple_of(xn[rel] * DS, DS), DS), :]
        else:
            weight = WP[pl.ds(pl.multiple_of(xn[rel] * DS, DS), DS), :]
        for b in range(3):
            r = pl.ds(b * 256, 256)
            part = dot(src[r, :], weight)
            acc[which, r, :] = part if first else acc[which, r, :] + part

    qs = (yh, 1 - yh)

    def gradient(rel, h):
        src = rows_of(rel)
        for b in range(2):
            cols = pl.ds(b * 256, 256)
            Pf[rel, h, cols, :] = tdot(src[:, cols], A[h]) + tdot(R[rel, :, cols], Rows[h])
        for k in range(4):
            theirs = pl.ds(pl.multiple_of((2 * k + 1 - c) * 64, 64), 64)
            Cs[rel, h, k * 64 : k * 64 + 64, :] = Pf[rel, h, theirs, :].astype(BF16)
        go(ccopy(rel, h))

    def ccopy(rel, h):
        return copy(Cs.at[rel, h], Cr.at[rel, h], cs.at[rel, h], cr.at[rel, h], mate)

    def zsend(rel, h):
        to = dev(z_=2 * xn[rel] + qs[h])
        return copy(Ss.at[rel, h], Zr.at[z], zs.at[rel, h], zr.at[z], to)

    def scatter(rel, h):
        ccopy(rel, h).wait_recv()
        for k in range(4):
            ours = pl.ds(pl.multiple_of((2 * k + c) * 64, 64), 64)
            part = slice(k * 64, k * 64 + 64)
            total = Pf[rel, h, ours, :] + Cr[rel, h, part, :].astype(F32)
            Ss[rel, h, part, :] = total.astype(BF16)

        @pl.when(2 * xn[rel] + qs[h] != z)
        def _():
            zsend(rel, h).start()

        @pl.when(2 * xn[rel] + qs[h] == z)
        def _():
            Zr[z] = Ss[rel, h]

    def pick(h):
        arows = tdot(oh[...], A[h]).astype(BF16)
        Rows[h, :MEM] = arows
        Rows[h, MEM:] = arows

    wfirst.wait_recv()

    wto = [zdev[1], zdev[7], dev(z_=lax.rem(z + 2 + 4 * c, 8))]

    def wspread(k, piece):
        return copy(WP.at[wpart(piece)], WP.at[wpart(piece)], wzs.at[k], wzr.at[k], wto[k])

    for k in range(3):
        go(wspread(k, 0))
    pick(0)
    gradient(0, 0)
    for k in range(XCH):
        own_right(k).wait_recv()
        go(on_right(k))
        own_left(k).wait_recv()
        go(on_left(k))
    rcopy(1).wait_recv()
    gradient(3, 0)
    rcopy(3).wait_recv()
    gradient(1, 0)
    for k, piece in enumerate((3, 1, 2)):
        wspread(k, piece).wait_recv()
    chalf = pl.ds(pl.multiple_of(c * 1024, 1024), 1024)
    ohalf = pl.ds(pl.multiple_of((1 - c) * 1024, 1024), 1024)
    go(copy(WP.at[chalf], WP.at[chalf], wc.at[0], wc.at[1], mate))
    scatter(0, 0)
    scatter(3, 0)
    scatter(1, 0)
    for load in loads[5:]:
        load.wait()
    for rel in (0, 3, 1):
        forward(rel, 0, rel == 0)
    copy(WP.at[ohalf], WP.at[ohalf], wc.at[0], wc.at[1], mate).wait_recv()
    for rel in (0, 3, 1):
        forward(rel, 1, rel == 0)
    rcopy(2).wait_recv()

    def change(which):
        total = None
        for rel in range(4):
            if which == 0:
                weight = w[pl.ds(pl.multiple_of(xn[rel] * DS, DS), DS), :]
            else:
                weight = WP[pl.ds(pl.multiple_of(xn[rel] * DS, DS), DS), :]
            part = dot(R[rel], weight)
            total = part if total is None else total + part
        return parts3(total[:MEM] + total[MEM:])

    def spread(rows, change3):
        o = oh[rows, :]
        return dot(o, change3[0]) + dot(o, change3[1]) + dot(o, change3[2])

    def part_far(j):
        r = pl.ds(j * YROWS, YROWS)
        return copy(Ps.at[r], Pr.at[r], ps.at[j], pr.at[j], far)

    theirs = change(1)
    weight = WP[pl.ds(pl.multiple_of(xn[2] * DS, DS), DS), :]
    for j in range(YCH):
        on_right(j).wait_recv()
        on_left(j).wait_recv()
        r = pl.ds(j * YROWS, YROWS)
        Ps[r, :] = (acc[1, r, :] + dot(G[1, r, :], weight) + spread(r, theirs)).astype(BF16)
        go(part_far(j))
    gradient(2, 0)
    forward(2, 0, False)
    scatter(2, 0)
    for j in range(YCH):
        attn_far(j).wait_recv()
    pick(1)
    gradient(0, 1)
    gradient(3, 1)
    scatter(0, 1)
    gradient(1, 1)
    scatter(3, 1)
    gradient(2, 1)
    scatter(1, 1)
    scatter(2, 1)
    ours = change(0)
    for j in range(YCH):
        r = pl.ds(j * YROWS, YROWS)
        acc[0, r, :] = acc[0, r, :] + spread(r, ours)
    for zz in range(8):
        @pl.when(zz != z)
        def _():
            copy(Zr.at[zz], Zr.at[zz], zs.at[0, 0], zr.at[zz], dev(z_=zz)).wait_recv()

    total = Zr[0].astype(F32)
    for zz in range(1, 8):
        total = total + Zr[zz].astype(F32)
    for k in range(4):
        Ys[k] = total[k * 64 : k * 64 + 64].astype(BF16)

    zf = jnp.where(straight, z, zx)
    yhf = jnp.where(straight, yh, 1 - yh)

    def ysend(k):
        there = lax.rem(yl + k, 4)
        return copy(Ys.at[there], Yr.at[yl], ys.at[k], yr.at[yl], dev(y_=4 * yhf + there, z_=zf))

    for k in range(1, 4):
        go(ysend(k))

    @pl.when(straight)
    def _():
        Yr[yl] = Ys[yl]

    @pl.when(jnp.logical_not(straight))
    def _():
        ysend(0).start()

    for j in range(YCH):
        part_far(j).wait_recv()
    oa[...] = (acc[0] + Pr[...].astype(F32)).astype(BF16)

    for k in range(1, 4):
        slot = lax.rem(yl + k, 4)
        copy(Ys.at[0], Yr.at[slot], ys.at[k], yr.at[slot], lo[k]).wait_recv()

    @pl.when(jnp.logical_not(straight))
    def _():
        d = ysend(0)
        d.wait_send()
        d.wait_recv()

    ow[...] = (Yr[0].astype(F32) + Yr[1].astype(F32)) + (Yr[2].astype(F32) + Yr[3].astype(F32))

    for d in sent:
        d.wait_send()
    for zz in range(7):
        @pl.when(zz < z)
        def _():
            copy(S3.at[z], S3.at[z], l3s.at[zz], l3r.at[z], dev(z_=zz)).wait_send()
    for rel in range(4):
        for h in range(2):
            @pl.when(2 * xn[rel] + qs[h] != z)
            def _():
                zsend(rel, h).wait_send()


def finish(a, b, c, oa, ow, om):
    oa[...] = a[...]
    ow[...] = b[...]
    om[...] = c[...]


def body(attn_out, out_proj_t, grad_out, read_weights, memory_gate, write_pos):
    vm, hb = pl.BlockSpec(memory_space=pltpu.VMEM), pl.BlockSpec(memory_space=pltpu.HBM)
    V, D = pltpu.VMEM, pltpu.SemaphoreType.DMA
    scratch = [
        V((T, DS), BF16), V((2048, HS), BF16), V((MEM, T), F32), V((MEM, MEM), F32),
        V((1, MEM), jnp.int32),
        V((3, T, DS), BF16), V((2, T, HS), BF16), V((2048, HS), BF16),
        V((2, MEM, DS + 128), F32), V((4, MEM, DS + 128), F32), V((8, MEM, DS + 128), F32),
        V((MEM, DS), F32), V((4, 2 * MEM, DS), BF16), V((2, 2 * MEM, HS), BF16),
        V((2, T, HS), F32), V((T, HS), BF16), V((T, HS), BF16),
        V((4, 2, DS, HS), F32), V((4, 2, 256, HS), BF16), V((4, 2, 256, HS), BF16),
        V((4, 2, 256, HS), BF16), V((8, 256, HS), BF16), V((4, 64, HS), BF16), V((4, 64, HS), BF16),
        V((T, MEM), BF16),
        D((9,)), D((2, XCH)), D((2, XCH)), D((2, XCH)), D((2, XCH)), D((YCH,)), D((YCH,)),
        D((2,)), D((8,)), D((8,)), D((2,)), D((2,)), D((4,)), D((4,)), D((8,)), D((8,)),
        D((4,)), D((4,)), D((YCH,)), D((YCH,)),
        D((4, 2)), D((4, 2)), D((4, 2)), D((8,)), D((4,)), D((4,)),
    ]
    shapes = (
        jax.ShapeDtypeStruct((T, HS), BF16),
        jax.ShapeDtypeStruct((64, HS), F32),
        jax.ShapeDtypeStruct((MEM, DS), F32),
    )
    results = pl.pallas_call(
        kernel,
        out_shape=shapes,
        in_specs=[hb] * 6,
        out_specs=(vm,) * 3,
        scratch_shapes=scratch,
        compiler_params=pltpu.CompilerParams(
            collective_id=0, has_side_effects=True, vmem_limit_bytes=40 * 1024 * 1024
        ),
    )(*[
        pltpu.with_memory_space_constraint(v, pltpu.HBM)
        for v in (grad_out, attn_out, out_proj_t, read_weights.T, memory_gate, write_pos)
    ])
    return pl.pallas_call(
        finish,
        out_shape=shapes,
        in_specs=[vm] * 3,
        out_specs=(vm,) * 3,
        compiler_params=pltpu.CompilerParams(vmem_limit_bytes=8 * 1024 * 1024),
    )(*results)


def solution(mesh):
    placed = (
        P("dp", "tensor"), P(None, "tensor"), P("dp", "tensor"),
        P("dp", None), P("dp", None), P("dp", None),
    )
    return jax.shard_map(
        body, mesh=mesh, in_specs=placed,
        out_specs=(P("dp", "tensor"), P("dp", "tensor"), P("dp", "tensor")), check_vma=False,
    )
```

time: 107 us -> 85 us (0.79)
  the two profiles are of different devices: /device:TPU:49 before, /device:TPU:184 now
where the time goes in v2:
time: 85 us; the launch traced here: 84.9 us
  Pallas kernels  84.2 us (99%)
    pallas_call x1, Pallas kernels, body(): pl.pallas_call(kernel, out_shape=shapes, in_specs=[hb] * 6, out_specs=(vm...  83.4 us

profile of v2, /device:TPU:184, one launch (start us, length us, event | category | flops | bytes accessed | tf_op | source)
XLA Modules:
  0.0 84.9 jit_solution(2649155535869650783)
XLA Ops:
  0.6 83.4 %shard_map.85 = (bf16[768,256]{1,0:T(8,128)(2,1)S(1)}, f32[64,256]{1,0:T(8,128)S(1)}, f32[16,512]{1,0:T(8,128)S(1)}) custom-call(bf16[768,512]{1,0:T(8,128)(2,1)} %g_in.1, bf16[768,256]{1,0:T(8,128)(2,1)} %attn.1, bf16[4096,256]{1,0:T(8,128)(2,1)} %w_in.1, f32[16,768]{1,0:T(8,128)} %bitcast.1, f32[16,16]{1,0:T(8,128)} %gate_in.1, s32[1,16]{1,0:T(1,128)} %wp_in.1), custom_call_target="tpu_custom_call" | custom-call | tf_op jit(solution)/shard_map/pallas_call | solution.py:438
  84.1 0.8 shard_map.86

commit v3 on v2

--- a/solution.py
+++ b/solution.py
@@ -41,7 +41,7 @@
     g_in, attn, w_in, rwt_in, gate_in, wp_in, oa, ow, om,
     g, w, rwt, gate, wp, G, A, WP, S1, S2, S3, vr, R, Rows, acc, Ps, Pr, Pf, Cs, Cr, Ss, Zr, Ys, Yr, oh,
     ins, xs, xr, fs, fr, ats, atr, w1, wzs, wzr, wc, l1, l2s, l2r, l3s, l3r, rs, rr,
-    ps, pr, cs, cr, zs, zr, ys, yr,
+    ps, pr, cs, cr, zs, zr, ys, yr, ygo,
 ):
     dp, tp = lax.axis_index("dp"), lax.axis_index("tensor")
     z, yl, c = lax.div(dp, 8), lax.rem(lax.div(dp, 2), 4), lax.rem(dp, 2)
@@ -65,6 +65,7 @@
     right, left, across = dev(x_=xn[1]), dev(x_=xn[3]), dev(x_=xn[2])
     yn = [lax.rem(y + k, 8) for k in range(8)]
     far = dev(y_=yn[4])
+    ring = [dev(y_=yn[k]) for k in range(1, 8)]
     mate = dev(c_=1 - c)
     lo = [dev(y_=4 * yh + lax.rem(yl + k, 4)) for k in range(4)]
     zn = [lax.rem(z + k, 8) for k in range(8)]
@@ -72,10 +73,10 @@
     odd = lax.rem(z, 2)
     zx = z + 1 - 2 * odd
     straight = odd == yh
-    cross = [dev(y_=4 * (1 - yh) + lax.rem(yl + k, 4), z_=zx) for k in range(4)]
+    cross = [dev(y_=yn[k], z_=zx) for k in range(8)]
 
     barrier = pltpu.get_barrier_semaphore()
-    greeted = [right, left, across, far, mate] + lo[1:] + zdev[1:] + cross
+    greeted = [right, left, across, mate] + ring + zdev[1:] + cross
     for peer in greeted:
         pl.semaphore_signal(barrier, inc=1, device_id=peer, device_id_type=pl.DeviceIdType.MESH)
 
@@ -139,9 +140,6 @@
         r = pl.ds(j * YROWS, YROWS)
         return copy(A.at[0, r], A.at[1, r], ats.at[j], atr.at[j], far)
 
-    for k in range(XCH):
-        go(own_right(k))
-        go(own_left(k))
     part = lax.rem(z, 4)
     wrow = pl.multiple_of(
         (2 * (2 * c + lax.div(part, 2)) + 1 - yh) * DS + lax.rem(part, 2) * 256, 256
@@ -163,10 +161,18 @@
     for k in range(1, 4):
         go(copy(S2.at[yl], S2.at[yl], l2s.at[k], l2r.at[yl], lo[k]))
     loads[4].wait()
+    go(wfirst)
+    for k in range(XCH):
+        go(own_right(k))
+        go(own_left(k))
     grows = tdot(oh[...], gv)
     for k in range(1, 4):
         slot = lax.rem(yl + k, 4)
         copy(S2.at[slot], S2.at[slot], l2s.at[k], l2r.at[slot], lo[k]).wait_recv()
+    for k in range(1, 8):
+        pl.semaphore_signal(
+            ygo, inc=1, device_id=ring[k - 1], device_id_type=pl.DeviceIdType.MESH
+        )
     term, mat = compose(S2[2], S2[3])
     for k in (1, 0):
         term, mat = compose(S2[k], jnp.concatenate([term, mat], axis=1))
@@ -177,10 +183,19 @@
         def _():
             copy(S3.at[z], S3.at[z], l3s.at[zz], l3r.at[z], dev(z_=zz)).start()
 
-    go(wfirst)
+
+    pl.semaphore_wait(ygo, 7)
     for j in range(YCH):
         go(attn_far(j))
-
+    wfirst.wait_recv()
+
+    wto = [zdev[1], zdev[7], dev(z_=lax.rem(z + 2 + 4 * c, 8))]
+
+    def wspread(k, piece):
+        return copy(WP.at[wpart(piece)], WP.at[wpart(piece)], wzs.at[k], wzr.at[k], wto[k])
+
+    for k in range(3):
+        go(wspread(k, 0))
     vr[...] = jnp.zeros((MEM, DS), F32)
 
     def through(s):
@@ -241,9 +256,13 @@
     def ccopy(rel, h):
         return copy(Cs.at[rel, h], Cr.at[rel, h], cs.at[rel, h], cr.at[rel, h], mate)
 
-    def zsend(rel, h):
-        to = dev(z_=2 * xn[rel] + qs[h])
-        return copy(Ss.at[rel, h], Zr.at[z], zs.at[rel, h], zr.at[z], to)
+    def zto(rel, h, r):
+        return 2 * xn[rel] + (qs[h] if r == 0 else 1 - qs[h])
+
+    def zsend(rel, h, r):
+        rows = pl.ds(r * 128, 128)
+        to = dev(z_=zto(rel, h, r))
+        return copy(Ss.at[rel, h, rows], Zr.at[z, r], zs.at[rel, h, r], zr.at[z, r], to)
 
     def scatter(rel, h):
         ccopy(rel, h).wait_recv()
@@ -252,29 +271,20 @@
             part = slice(k * 64, k * 64 + 64)
             total = Pf[rel, h, ours, :] + Cr[rel, h, part, :].astype(F32)
             Ss[rel, h, part, :] = total.astype(BF16)
-
-        @pl.when(2 * xn[rel] + qs[h] != z)
-        def _():
-            zsend(rel, h).start()
-
-        @pl.when(2 * xn[rel] + qs[h] == z)
-        def _():
-            Zr[z] = Ss[rel, h]
+        for r in range(2):
+            @pl.when(zto(rel, h, r) != z)
+            def _():
+                zsend(rel, h, r).start()
+
+            @pl.when(zto(rel, h, r) == z)
+            def _():
+                Zr[z, r] = Ss[rel, h, r * 128 : r * 128 + 128, :]
 
     def pick(h):
         arows = tdot(oh[...], A[h]).astype(BF16)
         Rows[h, :MEM] = arows
         Rows[h, MEM:] = arows
 
-    wfirst.wait_recv()
-
-    wto = [zdev[1], zdev[7], dev(z_=lax.rem(z + 2 + 4 * c, 8))]
-
-    def wspread(k, piece):
-        return copy(WP.at[wpart(piece)], WP.at[wpart(piece)], wzs.at[k], wzr.at[k], wto[k])
-
-    for k in range(3):
-        go(wspread(k, 0))
     pick(0)
     gradient(0, 0)
     for k in range(XCH):
@@ -351,45 +361,51 @@
     for zz in range(8):
         @pl.when(zz != z)
         def _():
-            copy(Zr.at[zz], Zr.at[zz], zs.at[0, 0], zr.at[zz], dev(z_=zz)).wait_recv()
+            for r in range(2):
+                copy(
+                    Zr.at[zz, r], Zr.at[zz, r], zs.at[0, 0, r], zr.at[zz, r], dev(z_=zz)
+                ).wait_recv()
 
     total = Zr[0].astype(F32)
     for zz in range(1, 8):
         total = total + Zr[zz].astype(F32)
     for k in range(4):
-        Ys[k] = total[k * 64 : k * 64 + 64].astype(BF16)
-
-    zf = jnp.where(straight, z, zx)
-    yhf = jnp.where(straight, yh, 1 - yh)
+        Ys[k] = total[k // 2, k % 2 * 64 : k % 2 * 64 + 64].astype(BF16)
+
+    zf = z - odd + yh
 
     def ysend(k):
-        there = lax.rem(yl + k, 4)
-        return copy(Ys.at[there], Yr.at[yl], ys.at[k], yr.at[yl], dev(y_=4 * yhf + there, z_=zf))
-
-    for k in range(1, 4):
-        go(ysend(k))
-
-    @pl.when(straight)
-    def _():
-        Yr[yl] = Ys[yl]
-
-    @pl.when(jnp.logical_not(straight))
-    def _():
-        ysend(0).start()
+        there = dev(y_=4 * (odd if k < 2 else 1 - odd) + k, z_=zf)
+        return copy(Ys.at[k], Yr.at[yl], ys.at[k], yr.at[yl], there)
+
+    def stays(k):
+        return jnp.logical_and(straight, yl == k)
+
+    for k in range(4):
+        if k < 2:
+            @pl.when(stays(k))
+            def _():
+                Yr[k] = Ys[k]
+
+            @pl.when(jnp.logical_not(stays(k)))
+            def _():
+                ysend(k).start()
+        else:
+            go(ysend(k))
 
     for j in range(YCH):
         part_far(j).wait_recv()
     oa[...] = (acc[0] + Pr[...].astype(F32)).astype(BF16)
 
-    for k in range(1, 4):
-        slot = lax.rem(yl + k, 4)
-        copy(Ys.at[0], Yr.at[slot], ys.at[k], yr.at[slot], lo[k]).wait_recv()
-
-    @pl.when(jnp.logical_not(straight))
-    def _():
-        d = ysend(0)
-        d.wait_send()
-        d.wait_recv()
+    for k in range(4):
+        come = copy(Ys.at[k], Yr.at[k], ys.at[k], yr.at[k], mate)
+        if k < 2:
+            @pl.when(jnp.logical_not(stays(k)))
+            def _():
+                come.wait_recv()
+                come.wait_send()
+        else:
+            come.wait_recv()
 
     ow[...] = (Yr[0].astype(F32) + Yr[1].astype(F32)) + (Yr[2].astype(F32) + Yr[3].astype(F32))
 
@@ -401,9 +417,10 @@
             copy(S3.at[z], S3.at[z], l3s.at[zz], l3r.at[z], dev(z_=zz)).wait_send()
     for rel in range(4):
         for h in range(2):
-            @pl.when(2 * xn[rel] + qs[h] != z)
-            def _():
-                zsend(rel, h).wait_send()
+            for r in range(2):
+                @pl.when(zto(rel, h, r) != z)
+                def _():
+                    zsend(rel, h, r).wait_send()
 
 
 def finish(a, b, c, oa, ow, om):
@@ -423,12 +440,12 @@
         V((MEM, DS), F32), V((4, 2 * MEM, DS), BF16), V((2, 2 * MEM, HS), BF16),
         V((2, T, HS), F32), V((T, HS), BF16), V((T, HS), BF16),
         V((4, 2, DS, HS), F32), V((4, 2, 256, HS), BF16), V((4, 2, 256, HS), BF16),
-        V((4, 2, 256, HS), BF16), V((8, 256, HS), BF16), V((4, 64, HS), BF16), V((4, 64, HS), BF16),
+        V((4, 2, 256, HS), BF16), V((8, 2, 128, HS), BF16), V((4, 64, HS), BF16), V((4, 64, HS), BF16),
         V((T, MEM), BF16),
         D((9,)), D((2, XCH)), D((2, XCH)), D((2, XCH)), D((2, XCH)), D((YCH,)), D((YCH,)),
         D((2,)), D((8,)), D((8,)), D((2,)), D((2,)), D((4,)), D((4,)), D((8,)), D((8,)),
         D((4,)), D((4,)), D((YCH,)), D((YCH,)),
-        D((4, 2)), D((4, 2)), D((4, 2)), D((8,)), D((4,)), D((4,)),
+        D((4, 2)), D((4, 2)), D((4, 2, 2)), D((8, 2)), D((4,)), D((4,)), pltpu.SemaphoreType.REGULAR,
     ]
     shapes = (
         jax.ShapeDtypeStruct((T, HS), BF16),

time: 85 us -> 78.8 us (0.927)
  the two profiles are of different devices: /device:TPU:184 before, /device:TPU:61 now
where the time goes in v3:
time: 78.8 us; the launch traced here: 78.1 us
  Pallas kernels  77.4 us (98%)
    pallas_call x1, Pallas kernels, body(): pl.pallas_call(kernel, out_shape=shapes, in_specs=[hb] * 6, out_specs=(vm...  76.6 us

profile of v3, /device:TPU:61, one launch (start us, length us, event | category | flops | bytes accessed | tf_op | source)
XLA Modules:
  0.0 78.1 jit_solution(11275631051022019007)
XLA Ops:
  0.6 76.6 %shard_map.85 = (bf16[768,256]{1,0:T(8,128)(2,1)S(1)}, f32[64,256]{1,0:T(8,128)S(1)}, f32[16,512]{1,0:T(8,128)S(1)}) custom-call(bf16[768,512]{1,0:T(8,128)(2,1)} %g_in.1, bf16[768,256]{1,0:T(8,128)(2,1)} %attn.1, bf16[4096,256]{1,0:T(8,128)(2,1)} %w_in.1, f32[16,768]{1,0:T(8,128)} %bitcast.1, f32[16,16]{1,0:T(8,128)} %gate_in.1, s32[1,16]{1,0:T(1,128)} %wp_in.1), custom_call_target="tpu_custom_call" | custom-call | tf_op jit(solution)/shard_map/pallas_call | solution.py:455
  77.3 0.8 %shard_map.86 = (bf16[768,256]{1,0:T(8,128)(2,1)}, f32[64,256]{1,0:T(8,128)}, f32[16,512]{1,0:T(8,128)}) custom-call(bf16[768,256]{1,0:T(8,128)(2,1)S(1)} %get-tuple-element.6.a, f32[64,256]{1,0:T(8,128)S(1)} %get-tuple-element.7.b, f32[16,512]{1,0:T(8,128)S(1)} %get-tuple-element.8.c), custom_call_target="tpu_custom_call" | custom-call | tf_op jit(solution)/shard_map/pallas_call | solution.py:468

commit v4 on v3

--- a/solution.py
+++ b/solution.py
@@ -8,6 +8,7 @@
 from jax.sharding import PartitionSpec as P
 
 T, DS, HS, MEM = 768, 512, 256, 16
+HC = DS // 2
 XCH, XROWS = 3, 256
 YCH, YROWS = 3, 256
 F32, BF16 = jnp.float32, jnp.bfloat16
@@ -39,8 +40,8 @@
 
 def kernel(
     g_in, attn, w_in, rwt_in, gate_in, wp_in, oa, ow, om,
-    g, w, rwt, gate, wp, G, A, WP, S1, S2, S3, vr, R, Rows, acc, Ps, Pr, Pf, Cs, Cr, Ss, Zr, Ys, Yr, oh,
-    ins, xs, xr, fs, fr, ats, atr, w1, wzs, wzr, wc, l1, l2s, l2r, l3s, l3r, rs, rr,
+    g, w, rwt, gate, wp, G, A, WP, S1, S2, S3, vr, Sx, Lo, Vx, Vr, Af, R, Rows, acc, Ps, Pr, Pf, Cs, Cr, Ss, Zr, Ys, Yr, oh,
+    ins, xs, xr, fs, fr, ats, atr, w1, wzs, wzr, wc, l1, vs, l2s, l2r, l3s, l3r, rs, rr,
     ps, pr, cs, cr, zs, zr, ys, yr, ygo,
 ):
     dp, tp = lax.axis_index("dp"), lax.axis_index("tensor")
@@ -101,12 +102,18 @@
         == lax.broadcasted_iota(jnp.int32, (MEM, 128), 1)
     ).astype(F32)
     loads[1].wait()
-    S1[c, :, DS:] = tdot(gate[...], eye, HIGH)
+    mat = tdot(gate[...], eye, HIGH)
+    S1[c, :, HC:] = mat
+    Sx[:, HC:] = mat
     loads[2].wait()
     hi, mid, low = parts3(rwt[...])
     loads[3].wait()
     gv = g[...]
-    S1[c, :, :DS] = dot(low, gv) + dot(mid, gv) + dot(hi, gv)
+    Lo[...] = dot(low, gv) + dot(mid, gv) + dot(hi, gv)
+    mycols = pl.ds(pl.multiple_of(c * HC, HC), HC)
+    matecols = pl.ds(pl.multiple_of((1 - c) * HC, HC), HC)
+    S1[c, :, :HC] = Lo[:, mycols]
+    Sx[:, :HC] = Lo[:, matecols]
     pl.semaphore_wait(barrier, len(greeted))
 
     sent = []
@@ -115,7 +122,7 @@
         d.start()
         sent.append(d)
 
-    lcopy = copy(S1.at[c], S1.at[c], l1.at[0], l1.at[1], mate)
+    lcopy = copy(Sx, S1.at[c], l1.at[0], l1.at[1], mate)
     go(lcopy)
 
     def own_right(k):
@@ -150,21 +157,22 @@
 
     wfirst = copy(w_in.at[pl.ds(wrow, 256)], WP.at[wpart(0)], w1.at[0], w1.at[1], far)
 
+    for k in range(XCH):
+        go(own_right(k))
+        go(own_left(k))
+
     def compose(early, late):
-        both = apply_map(early[:, DS:], late)
-        return both[:, :DS] + early[:, :DS], both[:, DS:]
+        both = apply_map(early[:, HC:], late)
+        return both[:, :HC] + early[:, :HC], both[:, HC:]
 
     lcopy.wait_recv()
     term, mat = compose(S1[0], S1[1])
-    S2[yl, :, :DS] = term
-    S2[yl, :, DS:] = mat
+    S2[yl, :, :HC] = term
+    S2[yl, :, HC:] = mat
     for k in range(1, 4):
         go(copy(S2.at[yl], S2.at[yl], l2s.at[k], l2r.at[yl], lo[k]))
     loads[4].wait()
     go(wfirst)
-    for k in range(XCH):
-        go(own_right(k))
-        go(own_left(k))
     grows = tdot(oh[...], gv)
     for k in range(1, 4):
         slot = lax.rem(yl + k, 4)
@@ -176,8 +184,8 @@
     term, mat = compose(S2[2], S2[3])
     for k in (1, 0):
         term, mat = compose(S2[k], jnp.concatenate([term, mat], axis=1))
-    S3[z, :, :DS] = term
-    S3[z, :, DS:] = mat
+    S3[z, :, :HC] = term
+    S3[z, :, HC:] = mat
     for zz in range(7):
         @pl.when(zz < z)
         def _():
@@ -196,10 +204,10 @@
 
     for k in range(3):
         go(wspread(k, 0))
-    vr[...] = jnp.zeros((MEM, DS), F32)
+    vr[...] = jnp.zeros((MEM, HC), F32)
 
     def through(s):
-        vr[...] = apply_map(s[:, DS:], vr[...]) + s[:, :DS]
+        vr[...] = apply_map(s[:, HC:], vr[...]) + s[:, :HC]
 
     for zz in range(7, 0, -1):
         @pl.when(zz > z)
@@ -212,13 +220,16 @@
         def _():
             through(S2[k])
 
-    @pl.when(c == 0)
-    def _():
-        through(S1[1])
-
-    after = vr[...]
-    mine = S1[c]
-    om[...] = apply_map(mine[:, DS:], after) + mine[:, :DS]
+    inner = apply_map(S1[1, :, HC:], vr[...]) + S1[1, :, :HC]
+    own = jnp.where(c == 0, inner, vr[...])
+    Vx[...] = jnp.where(c == 0, vr[...], inner)
+    vcopy = copy(Vx, Vr, vs.at[0], vs.at[1], mate)
+    go(vcopy)
+    Af[:, mycols] = own
+    vcopy.wait_recv()
+    Af[:, matecols] = Vr[...]
+    after = Af[...]
+    om[...] = apply_map(S1[c, :, HC:], after) + Lo[...]
     R[0, :MEM] = (grows + after).astype(BF16)
     R[0, MEM:] = (-grows).astype(BF16)
 
@@ -436,14 +447,15 @@
         V((T, DS), BF16), V((2048, HS), BF16), V((MEM, T), F32), V((MEM, MEM), F32),
         V((1, MEM), jnp.int32),
         V((3, T, DS), BF16), V((2, T, HS), BF16), V((2048, HS), BF16),
-        V((2, MEM, DS + 128), F32), V((4, MEM, DS + 128), F32), V((8, MEM, DS + 128), F32),
-        V((MEM, DS), F32), V((4, 2 * MEM, DS), BF16), V((2, 2 * MEM, HS), BF16),
+        V((2, MEM, HC + 128), F32), V((4, MEM, HC + 128), F32), V((8, MEM, HC + 128), F32),
+        V((MEM, HC), F32), V((MEM, HC + 128), F32), V((MEM, DS), F32), V((MEM, HC), F32),
+        V((MEM, HC), F32), V((MEM, DS), F32), V((4, 2 * MEM, DS), BF16), V((2, 2 * MEM, HS), BF16),
         V((2, T, HS), F32), V((T, HS), BF16), V((T, HS), BF16),
         V((4, 2, DS, HS), F32), V((4, 2, 256, HS), BF16), V((4, 2, 256, HS), BF16),
         V((4, 2, 256, HS), BF16), V((8, 2, 128, HS), BF16), V((4, 64, HS), BF16), V((4, 64, HS), BF16),
         V((T, MEM), BF16),
         D((9,)), D((2, XCH)), D((2, XCH)), D((2, XCH)), D((2, XCH)), D((YCH,)), D((YCH,)),
-        D((2,)), D((8,)), D((8,)), D((2,)), D((2,)), D((4,)), D((4,)), D((8,)), D((8,)),
+        D((2,)), D((8,)), D((8,)), D((2,)), D((2,)), D((2,)), D((4,)), D((4,)), D((8,)), D((8,)),
         D((4,)), D((4,)), D((YCH,)), D((YCH,)),
         D((4, 2)), D((4, 2)), D((4, 2, 2)), D((8, 2)), D((4,)), D((4,)), pltpu.SemaphoreType.REGULAR,
     ]

time: 78.8 us -> 77.2 us (0.980)
  Pallas kernels: 77.4 us -> 76.5 us
    pallas_call x1, Pallas kernels: 76.6 us -> 75.7 us  [body(): pl.pallas_call(kernel, out_shape=shapes, in_specs=[hb] * 6, out_specs=(vm...]
where the time goes in v4:
time: 77.2 us; the launch traced here: 77.1 us
  Pallas kernels  76.5 us (99%)
    pallas_call x1, Pallas kernels, body(): pl.pallas_call(kernel, out_shape=shapes, in_specs=[hb] * 6, out_specs=(vm...  75.7 us

profile of v4, /device:TPU:61, one launch (start us, length us, event | category | flops | bytes accessed | tf_op | source)
XLA Modules:
  0.0 77.1 jit_solution(2524710307812762789)
XLA Ops:
  0.6 75.7 %shard_map.85 = (bf16[768,256]{1,0:T(8,128)(2,1)S(1)}, f32[64,256]{1,0:T(8,128)S(1)}, f32[16,512]{1,0:T(8,128)S(1)}) custom-call(bf16[768,512]{1,0:T(8,128)(2,1)} %g_in.1, bf16[768,256]{1,0:T(8,128)(2,1)} %attn.1, bf16[4096,256]{1,0:T(8,128)(2,1)} %w_in.1, f32[16,768]{1,0:T(8,128)} %bitcast.1, f32[16,16]{1,0:T(8,128)} %gate_in.1, s32[1,16]{1,0:T(1,128)} %wp_in.1), custom_call_target="tpu_custom_call" | custom-call | tf_op jit(solution)/shard_map/pallas_call | solution.py:467
  76.3 0.8 %shard_map.86 = (bf16[768,256]{1,0:T(8,128)(2,1)}, f32[64,256]{1,0:T(8,128)}, f32[16,512]{1,0:T(8,128)}) custom-call(bf16[768,256]{1,0:T(8,128)(2,1)S(1)} %get-tuple-element.6.a, f32[64,256]{1,0:T(8,128)S(1)} %get-tuple-element.7.b, f32[16,512]{1,0:T(8,128)S(1)} %get-tuple-element.8.c), custom_call_target="tpu_custom_call" | custom-call | tf_op jit(solution)/shard_map/pallas_call | solution.py:480

commit v5 on v4

--- a/solution.py
+++ b/solution.py
@@ -202,7 +202,7 @@
     def wspread(k, piece):
         return copy(WP.at[wpart(piece)], WP.at[wpart(piece)], wzs.at[k], wzr.at[k], wto[k])
 
-    for k in range(3):
+    for k in (2, 0, 1):
         go(wspread(k, 0))
     vr[...] = jnp.zeros((MEM, HC), F32)
 
@@ -303,6 +303,7 @@
         go(on_right(k))
         own_left(k).wait_recv()
         go(on_left(k))
+    scatter(0, 0)
     rcopy(1).wait_recv()
     gradient(3, 0)
     rcopy(3).wait_recv()
@@ -312,7 +313,6 @@
     chalf = pl.ds(pl.multiple_of(c * 1024, 1024), 1024)
     ohalf = pl.ds(pl.multiple_of((1 - c) * 1024, 1024), 1024)
     go(copy(WP.at[chalf], WP.at[chalf], wc.at[0], wc.at[1], mate))
-    scatter(0, 0)
     scatter(3, 0)
     scatter(1, 0)
     for load in loads[5:]:

time: 77.2 us -> 77 us (level)
  no operation moved by 1% of the time
where the time goes in v5:
time: 77 us; the launch traced here: 76.9 us
  Pallas kernels  76.3 us (99%)
    pallas_call x1, Pallas kernels, body(): pl.pallas_call(kernel, out_shape=shapes, in_specs=[hb] * 6, out_specs=(vm...  75.5 us

profile of v5, /device:TPU:61, one launch (start us, length us, event | category | flops | bytes accessed | tf_op | source)
XLA Modules:
  0.0 76.9 jit_solution(1177423902470148388)
XLA Ops:
  0.6 75.5 %shard_map.85 = (bf16[768,256]{1,0:T(8,128)(2,1)S(1)}, f32[64,256]{1,0:T(8,128)S(1)}, f32[16,512]{1,0:T(8,128)S(1)}) custom-call(bf16[768,512]{1,0:T(8,128)(2,1)} %g_in.1, bf16[768,256]{1,0:T(8,128)(2,1)} %attn.1, bf16[4096,256]{1,0:T(8,128)(2,1)} %w_in.1, f32[16,768]{1,0:T(8,128)} %bitcast.1, f32[16,16]{1,0:T(8,128)} %gate_in.1, s32[1,16]{1,0:T(1,128)} %wp_in.1), custom_call_target="tpu_custom_call" | custom-call | tf_op jit(solution)/shard_map/pallas_call | solution.py:467
  76.1 0.8 %shard_map.86 = (bf16[768,256]{1,0:T(8,128)(2,1)}, f32[64,256]{1,0:T(8,128)}, f32[16,512]{1,0:T(8,128)}) custom-call(bf16[768,256]{1,0:T(8,128)(2,1)S(1)} %get-tuple-element.6.a, f32[64,256]{1,0:T(8,128)S(1)} %get-tuple-element.7.b, f32[16,512]{1,0:T(8,128)S(1)} %get-tuple-element.8.c), custom_call_target="tpu_custom_call" | custom-call | tf_op jit(solution)/shard_map/pallas_call | solution.py:480
